TPU v7x, 512 devices: a whole 4x8x8 slice. The times are simulated.
512 devices in a mesh: pts: 32 (over y, x), cen: 16 (over z, core).
Axes of the slice: x: 4, y: 8, z: 8, core: 2. Of those that a mesh axis runs over, the one named last changes fastest.
Arguments:
- points: bfloat16 [131072, 1024], P('pts'), may hold values from -60 to 60
- fine_assign: int32 [2, 131072], P(None, 'pts'), may hold values from 0 to 2047
- fine_start: float32 [2048, 1024], P('cen'), may hold values from -3 to 3
- coarse_start: float32 [64, 1024], replicated, may hold values from -3 to 3
- coarse_assign: int32 [2048], P('cen'), may hold values from 0 to 63
Outputs:
- fine_centroids: float32 [2048, 1024], P('cen')
- coarse_centroids: float32 [64, 1024], replicated
- gaps: float32 [2, 131072], P(None, 'pts')
All inputs are finite; a program needn't handle non-finite values.
Results may differ from a plain program's by a relative error of at most 0.0028.
Values sent between devices are 32-bit elements; how exact they have to be, the bound alone decides.
A program may use at most 64 MiB of HBM per device.

v0:
```python
import math
import jax
import jax.numpy as jnp
from jax import lax
from jax.sharding import PartitionSpec as P

NC = 64
PASSES = 2
prior_weight = 4.0


def copy_for_each(x, axis):
    size = lax.axis_size(axis)
    return lax.all_to_all(jnp.broadcast_to(x[None], (size, *x.shape)), axis, 0, 0, tiled=True)


def over_copies(x, axis):
    everything = copy_for_each(x, axis)
    return jnp.sum(everything, axis=0)


def over_copies_2(x, axis):
    everything = copy_for_each(x, axis)
    return jnp.min(everything, axis=0)


def in_blocks(x, dim, size):
    before, after = (x.shape[:dim], x.shape[dim + 1 :])
    return jnp.moveaxis(x.reshape(*before, size, -1, *after), dim, 0)


def sum_at_owner(x, axis, dim):
    blocks = in_blocks(x, dim, lax.axis_size(axis))
    arrived = lax.all_to_all(blocks, axis, split_axis=0, concat_axis=0, tiled=True)
    return arrived.sum(axis=0)


def in_one(arrays, axis):
    ends = [0]
    for a in arrays:
        ends.append(ends[-1] + a.size)
    running = over_copies(jnp.concatenate([a.ravel() for a in arrays]), axis)
    return tuple((running[b:e].reshape(a.shape) for a, b, e in zip(arrays, ends, ends[1:])))


def rows_first(arrays, axis, dims):
    turned = [jnp.moveaxis(a, dim, 0) for a, dim in zip(arrays, dims)]
    widths = [t[0].size for t in turned]
    both = jnp.concatenate([t.reshape(-1, w) for t, w in zip(turned, widths)], axis=1)
    filled = lax.all_gather(both, axis, axis=0, tiled=True)
    blocks = jnp.split(filled, [sum(widths[:k]) for k in range(1, len(widths))], axis=1)
    return tuple(
        (
            jnp.moveaxis(b.reshape(-1, *t.shape[1:]), 0, dim)
            for b, t, dim in zip(blocks, turned, dims)
        )
    )


def refine(totals, counts, coarse_cols, coarse_table):
    lookup = jnp.dot(coarse_table, coarse_cols, precision=lax.Precision.HIGHEST)
    fine_next = (totals + prior_weight * lookup) / (counts + prior_weight)[:, None]
    coarse_part = lax.dot_general(
        coarse_table,
        counts[:, None] * fine_next,
        (((0,), (0,)), ((), ())),
        precision=lax.Precision.HIGHEST,
    )
    coarse_weight = jnp.sum(coarse_table * counts[:, None], axis=0)
    return (fine_next, coarse_part, coarse_weight)


def on_device(points, fine_assign, fine_start, coarse_start, coarse_assign):
    width = points.shape[1]
    local_count = fine_start.shape[0]
    offset = lax.axis_index("cen") * local_count
    columns = jnp.arange(local_count, dtype=jnp.int32)
    coarse_table = (coarse_assign[:, None] == jnp.arange(NC, dtype=jnp.int32)[None, :]).astype(
        jnp.float32
    )
    point_values = points.astype(jnp.float32)
    squares = jnp.sum(point_values * point_values, axis=1)
    fine_now = fine_start
    coarse_now = coarse_start
    gap_rows = []
    for pass_index in range(PASSES):
        member = (fine_assign[pass_index] - offset)[:, None] == columns[None, :]
        products = jnp.dot(
            points, fine_now.astype(jnp.bfloat16).T, preferred_element_type=jnp.float32
        )
        energy = jnp.sum(fine_now * fine_now, axis=1)[None, :] - 2.0 * products
        picked_local = jnp.sum(jnp.where(member, energy, 0.0), axis=1)
        nearest_local = jnp.min(energy, axis=1)
        picked = over_copies(picked_local, "cen")
        nearest = over_copies_2(nearest_local, "cen")
        gap_rows.append((picked - nearest) / math.sqrt(width))
        weights = 1.0 / (1.0 + (squares + picked) / width)
        scaled = (point_values * weights[:, None]).astype(jnp.bfloat16)
        partial_sums = lax.dot_general(
            member.astype(jnp.bfloat16),
            scaled,
            (((0,), (0,)), ((), ())),
            preferred_element_type=jnp.float32,
        )
        partial_weights = jnp.sum(jnp.where(member, weights[:, None], 0.0), axis=0)
        share_width = width // lax.axis_size("pts")
        start = lax.axis_index("pts") * share_width
        shares = sum_at_owner(partial_sums, "pts", 1)
        counts = over_copies(partial_weights, "pts")
        coarse_cols = lax.dynamic_slice_in_dim(coarse_now, start, share_width, 1)
        fine_share, coarse_part, coarse_weight = refine(shares, counts, coarse_cols, coarse_table)
        coarse_sum, coarse_count = in_one((coarse_part, coarse_weight), "cen")
        coarse_share = (coarse_sum + prior_weight * coarse_cols) / (coarse_count + prior_weight)[
            :, None
        ]
        fine_now, coarse_now = rows_first((fine_share, coarse_share), "pts", (1, 1))
    return (fine_now, coarse_now, jnp.stack(gap_rows))


def solution(mesh):
    placed = (P("pts", None), P(None, "pts"), P("cen", None), P(), P("cen"))
    return jax.shard_map(
        on_device,
        mesh=mesh,
        in_specs=placed,
        out_specs=(P("cen", None), P(), P(None, "pts")),
        check_vma=False,
    )
```

profile of v0, /device:TPU:2, one launch (start us, length us, event | category | flops | bytes accessed | tf_op | source)
XLA Modules:
  0.0 298.8 jit_solution(10869809501321211903)
XLA Ops:
  0.6 1.2 multiply_reduce_fusion.1
  2.7 6.5 %fusion.33 = (f32[4096]{0:T(1024)S(1)}, f32[4096]{0:T(1024)S(1)}) fusion(s32[4096]{0:T(1024)S(1)} %bitcast.44, bf16[4096,1024]{1,0:T(8,128)(2,1)} %param.5, f32[128,1024]{1,0:T(8,128)} %param.7, f32[128]{0:T(128)S(1)} %multiply_reduce_fusion.1), kind=kOutput, calls=%fused_computation.70 | convolution fusion | flops 1077010432 | bytes 8962560 | tf_op jit(solution)/shard_map/dot_general | solution.py:88
  9.4 21.4 %all_to_all.58 = f32[16,1,4096]{2,1,0:T(1,128)S(1)} all-to-all(f32[16,1,4096]{2,1,0:T(1,128)S(1)} %broadcast_in_dim.46), channel_id=1, replica_groups=mesh['pts'=32,'cen'=16] {'cen'}, dimensions={0} | all-to-all | bytes 524288 | tf_op jit(solution)/shard_map/all_to_all | solution.py:14
  31.7 3.5 %all-to-all-start = ((f32[16,1,4096]{2,1,0:T(1,128)}), f32[16,1,4096]{2,1,0:T(1,128)S(1)}, u32[]{:S(2)}, u32[]{:S(2)}) async-start(f32[16,1,4096]{2,1,0:T(1,128)} %broadcast_in_dim.38), calls=%async_computation | async-start | bytes 524288 | tf_op jit(solution)/shard_map/all_to_all | solution.py:14
  35.2 5.1 %fusion = f32[4096]{0:T(1024)S(1)} fusion(bf16[4096,1024]{1,0:T(8,128)(2,1)} %param.5), kind=kLoop, calls=%fused_computation.3 | loop fusion | flops 12578816 | bytes 8404992 | tf_op jit(solution)/shard_map/reduce_sum | solution.py:82
  40.5 6.0 %all-to-all-done = f32[16,1,4096]{2,1,0:T(1,128)S(1)} async-done(((f32[16,1,4096]{2,1,0:T(1,128)}), f32[16,1,4096]{2,1,0:T(1,128)S(1)}, u32[]{:S(2)}, u32[]{:S(2)}) %all-to-all-start) | async-done | bytes 262176 | tf_op jit(solution)/shard_map/all_to_all | solution.py:14
  47.7 10.2 %all-to-all-start.2 = ((f32[32,1,128]{2,1,0:T(1,128)}), f32[32,1,128]{2,1,0:T(1,128)S(1)}, u32[]{:S(2)}, u32[]{:S(2)}) async-start(f32[32,1,128]{2,1,0:T(1,128)} %broadcast_in_dim.40), calls=%async_computation.2 | async-start | bytes 32768 | tf_op jit(solution)/shard_map/all_to_all | solution.py:14
  58.0 8.1 %fusion.5 = f32[128,1024]{0,1:T(8,128)} fusion(bf16[4096,1024]{1,0:T(8,128)(2,1)} %param.5, f32[4096]{0:T(1024)S(1)} %get-tuple-element.20, s32[4096]{0:T(1024)S(1)} %bitcast.46), kind=kOutput, calls=%fused_computation.7 | convolution fusion | flops 1086849024 | bytes 8945664 | tf_op jit(solution)/shard_map/dot_general | solution.py:99
  66.5 9.4 %all-to-all-start.1 = ((f32[32,128,32]{1,2,0:T(8,128)}), f32[32,128,32]{1,2,0:T(8,128)S(1)}, u32[]{:S(2)}, u32[]{:S(2)}) async-start(f32[32,128,32]{1,2,0:T(8,128)} %bitcast.3), calls=%async_computation.1 | async-start | bytes 1048576 | tf_op jit(solution)/shard_map/all_to_all | solution.py:34
  76.1 16.8 %all-to-all-done.1 = f32[32,128,32]{1,2,0:T(8,128)S(1)} async-done(((f32[32,128,32]{1,2,0:T(8,128)}), f32[32,128,32]{1,2,0:T(8,128)S(1)}, u32[]{:S(2)}, u32[]{:S(2)}) %all-to-all-start.1) | async-done | bytes 524320 | tf_op jit(solution)/shard_map/all_to_all | solution.py:34
  94.1 3.5 %all-to-all-start.3 = ((f32[16,1,2112]{2,1,0:T(1,128)}), f32[16,1,2112]{2,1,0:T(1,128)S(1)}, u32[]{:S(2)}, u32[]{:S(2)}) async-start(f32[16,1,2112]{2,1,0:T(1,128)} %broadcast_in_dim.41), calls=%async_computation.3 | async-start | bytes 278528 | tf_op jit(solution)/shard_map/all_to_all | solution.py:14
  97.7 8.7 %all-to-all-done.3 = f32[16,1,2112]{2,1,0:T(1,128)S(1)} async-done(((f32[16,1,2112]{2,1,0:T(1,128)}), f32[16,1,2112]{2,1,0:T(1,128)S(1)}, u32[]{:S(2)}, u32[]{:S(2)}) %all-to-all-start.3) | async-done | bytes 135200 | tf_op jit(solution)/shard_map/all_to_all | solution.py:14
  106.7 48.5 %all_gather.6 = f32[1024,192]{1,0:T(8,128)S(1)} all-gather(f32[32,192]{1,0:T(8,128)S(1)} %pad_maximum_fusion), channel_id=1, replica_groups=mesh['pts'=32,'cen'=16] {'pts'}, dimensions={0}, use_global_device_ids=true | all-gather | bytes 811008 | tf_op jit(solution)/shard_map/all_gather | solution.py:50
  155.4 6.5 %fusion.11 = (f32[4096]{0:T(1024)S(1)}, f32[128,4096]{1,0:T(8,128)S(1)}) fusion(s32[4096]{0:T(1024)S(1)} %bitcast.35, bf16[4096,1024]{1,0:T(8,128)(2,1)} %param.5, f32[1024,192]{1,0:T(8,128)S(1)} %all_gather.6, f32[128]{0:T(128)S(1)} %multiply_reduce_fusion), kind=kOutput, calls=%fused_computation.15 | convolution fusion | flops 1076359168 | bytes 10781184 | tf_op jit(solution)/shard_map/dot_general | solution.py:88
  162.2 14.1 %all_to_all.59 = f32[16,1,4096]{2,1,0:T(1,128)S(1)} all-to-all(f32[16,1,4096]{2,1,0:T(1,128)S(1)} %broadcast_in_dim.47), channel_id=1, replica_groups=mesh['pts'=32,'cen'=16] {'cen'}, dimensions={0} | all-to-all | bytes 524288 | tf_op jit(solution)/shard_map/all_to_all | solution.py:14
  177.2 3.5 %all-to-all-start.4 = ((f32[16,1,4096]{2,1,0:T(1,128)}), f32[16,1,4096]{2,1,0:T(1,128)S(1)}, u32[]{:S(2)}, u32[]{:S(2)}) async-start(f32[16,1,4096]{2,1,0:T(1,128)} %broadcast_in_dim.42), calls=%async_computation.4 | async-start | bytes 524288 | tf_op jit(solution)/shard_map/all_to_all | solution.py:14
  180.9 11.1 %all-to-all-done.4 = f32[16,1,4096]{2,1,0:T(1,128)S(1)} async-done(((f32[16,1,4096]{2,1,0:T(1,128)}), f32[16,1,4096]{2,1,0:T(1,128)S(1)}, u32[]{:S(2)}, u32[]{:S(2)}) %all-to-all-start.4) | async-done | bytes 262176 | tf_op jit(solution)/shard_map/all_to_all | solution.py:14
  193.2 6.6 %all-to-all-start.6 = ((f32[32,1,128]{2,1,0:T(1,128)}), f32[32,1,128]{2,1,0:T(1,128)S(1)}, u32[]{:S(2)}, u32[]{:S(2)}) async-start(f32[32,1,128]{2,1,0:T(1,128)} %broadcast_in_dim.44), calls=%async_computation.6 | async-start | bytes 32768 | tf_op jit(solution)/shard_map/all_to_all | solution.py:14
  199.9 8.1 %fusion.3 = f32[128,1024]{0,1:T(8,128)} fusion(bf16[4096,1024]{1,0:T(8,128)(2,1)} %param.5, f32[4096]{0:T(1024)S(1)} %get-tuple-element.22, s32[4096]{0:T(1024)S(1)} %bitcast.37), kind=kOutput, calls=%fused_computation.6 | convolution fusion | flops 1086849024 | bytes 8945664 | tf_op jit(solution)/shard_map/dot_general | solution.py:99
  208.3 9.4 %all-to-all-start.5 = ((f32[32,128,32]{1,2,0:T(8,128)}), f32[32,128,32]{1,2,0:T(8,128)S(1)}, u32[]{:S(2)}, u32[]{:S(2)}) async-start(f32[32,128,32]{1,2,0:T(8,128)} %bitcast.9), calls=%async_computation.5 | async-start | bytes 1048576 | tf_op jit(solution)/shard_map/all_to_all | solution.py:34
  217.9 16.8 %all-to-all-done.5 = f32[32,128,32]{1,2,0:T(8,128)S(1)} async-done(((f32[32,128,32]{1,2,0:T(8,128)}), f32[32,128,32]{1,2,0:T(8,128)S(1)}, u32[]{:S(2)}, u32[]{:S(2)}) %all-to-all-start.5) | async-done | bytes 524320 | tf_op jit(solution)/shard_map/all_to_all | solution.py:34
  235.9 3.5 %all-to-all-start.7 = ((f32[16,1,2112]{2,1,0:T(1,128)}), f32[16,1,2112]{2,1,0:T(1,128)S(1)}, u32[]{:S(2)}, u32[]{:S(2)}) async-start(f32[16,1,2112]{2,1,0:T(1,128)} %broadcast_in_dim.45), calls=%async_computation.7 | async-start | bytes 278528 | tf_op jit(solution)/shard_map/all_to_all | solution.py:14
  240.1 8.1 %all-to-all-done.7 = f32[16,1,2112]{2,1,0:T(1,128)S(1)} async-done(((f32[16,1,2112]{2,1,0:T(1,128)}), f32[16,1,2112]{2,1,0:T(1,128)S(1)}, u32[]{:S(2)}, u32[]{:S(2)}) %all-to-all-start.7) | async-done | bytes 135200 | tf_op jit(solution)/shard_map/all_to_all | solution.py:14
  248.5 48.3 %all_gather.7 = f32[1024,192]{1,0:T(8,128)S(1)} all-gather(f32[32,192]{1,0:T(8,128)S(1)} %pad_maximum_fusion.1), channel_id=1, replica_groups=mesh['pts'=32,'cen'=16] {'pts'}, dimensions={0}, use_global_device_ids=true | all-gather | bytes 811008 | tf_op jit(solution)/shard_map/all_gather | solution.py:50
  (63 shorter events, 12.7 us)
Async XLA Ops:
  0.6 75.3 %copy-start = (f32[64,1024]{1,0:T(8,128)S(1)}, f32[64,1024]{1,0:T(8,128)}, u32[]{:S(2)}) copy-start(f32[64,1024]{1,0:T(8,128)} %param.8) | copy-start | bytes 786436
  31.7 14.9 %all-to-all-start = ((f32[16,1,4096]{2,1,0:T(1,128)}), f32[16,1,4096]{2,1,0:T(1,128)S(1)}, u32[]{:S(2)}, u32[]{:S(2)}) async-start(f32[16,1,4096]{2,1,0:T(1,128)} %broadcast_in_dim.38), calls=%async_computation | async-start | bytes 524288 | tf_op jit(solution)/shard_map/all_to_all | solution.py:14
  47.7 18.7 %all-to-all-start.2 = ((f32[32,1,128]{2,1,0:T(1,128)}), f32[32,1,128]{2,1,0:T(1,128)S(1)}, u32[]{:S(2)}, u32[]{:S(2)}) async-start(f32[32,1,128]{2,1,0:T(1,128)} %broadcast_in_dim.40), calls=%async_computation.2 | async-start | bytes 32768 | tf_op jit(solution)/shard_map/all_to_all | solution.py:14
  58.0 18.0 %copy-start.1 = (s32[128]{0:T(128)S(1)}, s32[128]{0:T(128)}, u32[]{:S(2)}) copy-start(s32[128]{0:T(128)} %param.9) | copy-start | bytes 1540
  66.5 26.4 %all-to-all-start.1 = ((f32[32,128,32]{1,2,0:T(8,128)}), f32[32,128,32]{1,2,0:T(8,128)S(1)}, u32[]{:S(2)}, u32[]{:S(2)}) async-start(f32[32,128,32]{1,2,0:T(8,128)} %bitcast.3), calls=%async_computation.1 | async-start | bytes 1048576 | tf_op jit(solution)/shard_map/all_to_all | solution.py:34
  94.1 12.3 %all-to-all-start.3 = ((f32[16,1,2112]{2,1,0:T(1,128)}), f32[16,1,2112]{2,1,0:T(1,128)S(1)}, u32[]{:S(2)}, u32[]{:S(2)}) async-start(f32[16,1,2112]{2,1,0:T(1,128)} %broadcast_in_dim.41), calls=%async_computation.3 | async-start | bytes 278528 | tf_op jit(solution)/shard_map/all_to_all | solution.py:14
  177.2 14.9 %all-to-all-start.4 = ((f32[16,1,4096]{2,1,0:T(1,128)}), f32[16,1,4096]{2,1,0:T(1,128)S(1)}, u32[]{:S(2)}, u32[]{:S(2)}) async-start(f32[16,1,4096]{2,1,0:T(1,128)} %broadcast_in_dim.42), calls=%async_computation.4 | async-start | bytes 524288 | tf_op jit(solution)/shard_map/all_to_all | solution.py:14
  193.2 15.1 %all-to-all-start.6 = ((f32[32,1,128]{2,1,0:T(1,128)}), f32[32,1,128]{2,1,0:T(1,128)S(1)}, u32[]{:S(2)}, u32[]{:S(2)}) async-start(f32[32,1,128]{2,1,0:T(1,128)} %broadcast_in_dim.44), calls=%async_computation.6 | async-start | bytes 32768 | tf_op jit(solution)/shard_map/all_to_all | solution.py:14
  208.3 26.4 %all-to-all-start.5 = ((f32[32,128,32]{1,2,0:T(8,128)}), f32[32,128,32]{1,2,0:T(8,128)S(1)}, u32[]{:S(2)}, u32[]{:S(2)}) async-start(f32[32,128,32]{1,2,0:T(8,128)} %bitcast.9), calls=%async_computation.5 | async-start | bytes 1048576 | tf_op jit(solution)/shard_map/all_to_all | solution.py:34
  235.9 12.3 %all-to-all-start.7 = ((f32[16,1,2112]{2,1,0:T(1,128)}), f32[16,1,2112]{2,1,0:T(1,128)S(1)}, u32[]{:S(2)}, u32[]{:S(2)}) async-start(f32[16,1,2112]{2,1,0:T(1,128)} %broadcast_in_dim.45), calls=%async_computation.7 | async-start | bytes 278528 | tf_op jit(solution)/shard_map/all_to_all | solution.py:14
where the time goes:
time: 300 us; the launch traced here: 299 us
  blocking collectives  132 us (44%)
  waiting for transfers between devices  68.4 us (23%)
  starting transfers between devices  49.8 us (17%)
  matrix products  29.8 us (10%)
  other arithmetic  10.1 us (3%)
  local copies, waits for them, and re-layouts  7.5 us (2%)
    all_gather x2, blocking collectives, rows_first(): filled = lax.all_gather(both, axis, axis=0, tiled=True)  96.8 us
    all_to_all x2, blocking collectives, copy_for_each(): lax.all_to_all(jnp.broadcast_to(x[None], (size, *x.shape)), axis, 0, 0, t...  35.5 us
    all_to_all x6, waiting for transfers between devices, copy_for_each(): lax.all_to_all(jnp.broadcast_to(x[None], (size, *x.shape)), axis, 0, 0, t...  34.8 us
    all_to_all x2, waiting for transfers between devices, sum_at_owner(): lax.all_to_all(blocks, axis, split_axis=0, concat_axis=0, tiled=True)  33.6 us
    all_to_all x6, starting transfers between devices, copy_for_each(): lax.all_to_all(jnp.broadcast_to(x[None], (size, *x.shape)), axis, 0, 0, t...  31 us
    all_to_all x2, starting transfers between devices, sum_at_owner(): lax.all_to_all(blocks, axis, split_axis=0, concat_axis=0, tiled=True)  18.8 us
    dot_general x2, matrix products, on_device(): lax.dot_general(member.astype(jnp.bfloat16), scaled, (((0,), (0,)), ((),...  16.2 us
    dot_general x2, matrix products, on_device(): jnp.dot(points, fine_now.astype(jnp.bfloat16).T, preferred_element_type=j...  13 us
  transfers between devices with their start and end apart: 8, of which 8 were waited for; matrix products, arithmetic and copies ran while one was open for 8% of the time, Pallas kernels for 0%

commit v1 on v0

--- a/solution.py
+++ b/solution.py
@@ -47,7 +47,9 @@
     turned = [jnp.moveaxis(a, dim, 0) for a, dim in zip(arrays, dims)]
     widths = [t[0].size for t in turned]
     both = jnp.concatenate([t.reshape(-1, w) for t, w in zip(turned, widths)], axis=1)
-    filled = lax.all_gather(both, axis, axis=0, tiled=True)
+    filled = jnp.concatenate(
+        lax.all_to_all(jnp.stack([both] * lax.axis_size(axis)), axis, 0, 0), axis=0
+    )
     blocks = jnp.split(filled, [sum(widths[:k]) for k in range(1, len(widths))], axis=1)
     return tuple(
         (

time: 300 us -> 270 us (0.900)
  blocking collectives: 132 us -> 80.8 us
  waiting for transfers between devices: 68.4 us -> 88.4 us
    all_gather x2 -> x0, blocking collectives: 96.8 us -> none  [rows_first(): filled = lax.all_gather(both, axis, axis=0, tiled=True)]
    all_to_all x0 -> x1, blocking collectives: none -> 34.5 us  [rows_first(): lax.all_to_all(jnp.stack([both] * lax.axis_size(axis)), axis, 0, 0)]
    all_to_all x0 -> x1, waiting for transfers between devices: none -> 28.2 us  [rows_first(): lax.all_to_all(jnp.stack([both] * lax.axis_size(axis)), axis, 0, 0)]
    all_to_all x2 -> x3, blocking collectives: 35.5 us -> 46.3 us  [copy_for_each(): lax.all_to_all(jnp.broadcast_to(x[None], (size, *x.shape)), axis, 0, 0, t...]
    all_to_all x6 -> x5, waiting for transfers between devices: 34.8 us -> 26.7 us  [copy_for_each(): lax.all_to_all(jnp.broadcast_to(x[None], (size, *x.shape)), axis, 0, 0, t...]
    all_to_all x0 -> x1, starting transfers between devices: none -> 5.57 us  [rows_first(): lax.all_to_all(jnp.stack([both] * lax.axis_size(axis)), axis, 0, 0)]
    all_to_all x6 -> x5, starting transfers between devices: 31 us -> 26.4 us  [copy_for_each(): lax.all_to_all(jnp.broadcast_to(x[None], (size, *x.shape)), axis, 0, 0, t...]
where the time goes in v1:
time: 270 us; the launch traced here: 269 us
  waiting for transfers between devices  88.4 us (33%)
  blocking collectives  80.8 us (30%)
  starting transfers between devices  50.8 us (19%)
  matrix products  29.8 us (11%)
  other arithmetic  10.1 us (4%)
  local copies, waits for them, and re-layouts  8.06 us (3%)
    all_to_all x3, blocking collectives, copy_for_each(): lax.all_to_all(jnp.broadcast_to(x[None], (size, *x.shape)), axis, 0, 0, t...  46.3 us
    all_to_all x1, blocking collectives, rows_first(): lax.all_to_all(jnp.stack([both] * lax.axis_size(axis)), axis, 0, 0)  34.5 us
    all_to_all x2, waiting for transfers between devices, sum_at_owner(): lax.all_to_all(blocks, axis, split_axis=0, concat_axis=0, tiled=True)  33.6 us
    all_to_all x1, waiting for transfers between devices, rows_first(): lax.all_to_all(jnp.stack([both] * lax.axis_size(axis)), axis, 0, 0)  28.2 us
    all_to_all x5, waiting for transfers between devices, copy_for_each(): lax.all_to_all(jnp.broadcast_to(x[None], (size, *x.shape)), axis, 0, 0, t...  26.7 us
    all_to_all x5, starting transfers between devices, copy_for_each(): lax.all_to_all(jnp.broadcast_to(x[None], (size, *x.shape)), axis, 0, 0, t...  26.4 us
    all_to_all x2, starting transfers between devices, sum_at_owner(): lax.all_to_all(blocks, axis, split_axis=0, concat_axis=0, tiled=True)  18.8 us
    dot_general x2, matrix products, on_device(): lax.dot_general(member.astype(jnp.bfloat16), scaled, (((0,), (0,)), ((),...  16.2 us
  transfers between devices with their start and end apart: 8, of which 8 were waited for; matrix products, arithmetic and copies ran while one was open for 8% of the time, Pallas kernels for 0%

profile of v1, /device:TPU:2, one launch (start us, length us, event | category | flops | bytes accessed | tf_op | source)
XLA Modules:
  0.0 269.0 jit_solution(14290968520032491625)
XLA Ops:
  0.6 1.2 multiply_reduce_fusion.1
  2.7 6.5 %fusion.33 = (f32[4096]{0:T(1024)S(1)}, f32[4096]{0:T(1024)S(1)}) fusion(s32[4096]{0:T(1024)S(1)} %bitcast.51, bf16[4096,1024]{1,0:T(8,128)(2,1)} %param.5, f32[128,1024]{1,0:T(8,128)} %param.7, f32[128]{0:T(128)S(1)} %multiply_reduce_fusion.1), kind=kOutput, calls=%fused_computation.70 | convolution fusion | flops 1077010432 | bytes 8962560 | tf_op jit(solution)/shard_map/dot_general | solution.py:90
  9.4 21.4 %all_to_all.68 = f32[16,1,4096]{2,1,0:T(1,128)S(1)} all-to-all(f32[16,1,4096]{2,1,0:T(1,128)S(1)} %broadcast_in_dim.46), channel_id=1, replica_groups=mesh['pts'=32,'cen'=16] {'cen'}, dimensions={0} | all-to-all | bytes 524288 | tf_op jit(solution)/shard_map/all_to_all | solution.py:14
  31.7 3.5 %all-to-all-start = ((f32[16,1,4096]{2,1,0:T(1,128)}), f32[16,1,4096]{2,1,0:T(1,128)S(1)}, u32[]{:S(2)}, u32[]{:S(2)}) async-start(f32[16,1,4096]{2,1,0:T(1,128)} %broadcast_in_dim.38), calls=%async_computation | async-start | bytes 524288 | tf_op jit(solution)/shard_map/all_to_all | solution.py:14
  35.2 5.1 %fusion = f32[4096]{0:T(1024)S(1)} fusion(bf16[4096,1024]{1,0:T(8,128)(2,1)} %param.5), kind=kLoop, calls=%fused_computation.3 | loop fusion | flops 12578816 | bytes 8404992 | tf_op jit(solution)/shard_map/reduce_sum | solution.py:84
  40.5 6.0 %all-to-all-done = f32[16,1,4096]{2,1,0:T(1,128)S(1)} async-done(((f32[16,1,4096]{2,1,0:T(1,128)}), f32[16,1,4096]{2,1,0:T(1,128)S(1)}, u32[]{:S(2)}, u32[]{:S(2)}) %all-to-all-start) | async-done | bytes 262176 | tf_op jit(solution)/shard_map/all_to_all | solution.py:14
  47.7 10.2 %all-to-all-start.2 = ((f32[32,1,128]{2,1,0:T(1,128)}), f32[32,1,128]{2,1,0:T(1,128)S(1)}, u32[]{:S(2)}, u32[]{:S(2)}) async-start(f32[32,1,128]{2,1,0:T(1,128)} %broadcast_in_dim.40), calls=%async_computation.2 | async-start | bytes 32768 | tf_op jit(solution)/shard_map/all_to_all | solution.py:14
  58.0 8.1 %fusion.5 = f32[128,1024]{0,1:T(8,128)} fusion(bf16[4096,1024]{1,0:T(8,128)(2,1)} %param.5, f32[4096]{0:T(1024)S(1)} %get-tuple-element.17, s32[4096]{0:T(1024)S(1)} %bitcast.53), kind=kOutput, calls=%fused_computation.7 | convolution fusion | flops 1086849024 | bytes 8945664 | tf_op jit(solution)/shard_map/dot_general | solution.py:101
  66.5 9.4 %all-to-all-start.1 = ((f32[32,128,32]{1,2,0:T(8,128)}), f32[32,128,32]{1,2,0:T(8,128)S(1)}, u32[]{:S(2)}, u32[]{:S(2)}) async-start(f32[32,128,32]{1,2,0:T(8,128)} %bitcast.3), calls=%async_computation.1 | async-start | bytes 1048576 | tf_op jit(solution)/shard_map/all_to_all | solution.py:34
  76.1 16.8 %all-to-all-done.1 = f32[32,128,32]{1,2,0:T(8,128)S(1)} async-done(((f32[32,128,32]{1,2,0:T(8,128)}), f32[32,128,32]{1,2,0:T(8,128)S(1)}, u32[]{:S(2)}, u32[]{:S(2)}) %all-to-all-start.1) | async-done | bytes 524320 | tf_op jit(solution)/shard_map/all_to_all | solution.py:34
  94.1 3.5 %all-to-all-start.3 = ((f32[16,1,2112]{2,1,0:T(1,128)}), f32[16,1,2112]{2,1,0:T(1,128)S(1)}, u32[]{:S(2)}, u32[]{:S(2)}) async-start(f32[16,1,2112]{2,1,0:T(1,128)} %broadcast_in_dim.41), calls=%async_computation.3 | async-start | bytes 278528 | tf_op jit(solution)/shard_map/all_to_all | solution.py:14
  97.7 8.7 %all-to-all-done.3 = f32[16,1,2112]{2,1,0:T(1,128)S(1)} async-done(((f32[16,1,2112]{2,1,0:T(1,128)}), f32[16,1,2112]{2,1,0:T(1,128)S(1)}, u32[]{:S(2)}, u32[]{:S(2)}) %all-to-all-start.3) | async-done | bytes 135200 | tf_op jit(solution)/shard_map/all_to_all | solution.py:14
  106.8 34.5 %all_to_all.69 = f32[32,32,192]{2,1,0:T(8,128)S(1)} all-to-all(f32[32,32,192]{2,1,0:T(8,128)S(1)} %stack.6), channel_id=1, replica_groups=mesh['pts'=32,'cen'=16] {'pts'}, dimensions={0} | all-to-all | bytes 1572864 | tf_op jit(solution)/shard_map/all_to_all | solution.py:51
  141.5 6.5 %fusion.11 = (f32[4096]{0:T(1024)S(1)}, f32[128,4096]{1,0:T(8,128)S(1)}) fusion(s32[4096]{0:T(1024)S(1)} %bitcast.42, bf16[4096,1024]{1,0:T(8,128)(2,1)} %param.5, f32[1024,192]{1,0:T(8,128)S(1)} %bitcast.38, f32[128]{0:T(128)S(1)} %multiply_reduce_fusion), kind=kOutput, calls=%fused_computation.15 | convolution fusion | flops 1076359168 | bytes 10781184 | tf_op jit(solution)/shard_map/dot_general | solution.py:90
  148.3 13.6 %all_to_all.70 = f32[16,1,4096]{2,1,0:T(1,128)S(1)} all-to-all(f32[16,1,4096]{2,1,0:T(1,128)S(1)} %broadcast_in_dim.47), channel_id=1, replica_groups=mesh['pts'=32,'cen'=16] {'cen'}, dimensions={0} | all-to-all | bytes 524288 | tf_op jit(solution)/shard_map/all_to_all | solution.py:14
  162.8 3.5 %all-to-all-start.5 = ((f32[16,1,4096]{2,1,0:T(1,128)}), f32[16,1,4096]{2,1,0:T(1,128)S(1)}, u32[]{:S(2)}, u32[]{:S(2)}) async-start(f32[16,1,4096]{2,1,0:T(1,128)} %broadcast_in_dim.42), calls=%async_computation.5 | async-start | bytes 524288 | tf_op jit(solution)/shard_map/all_to_all | solution.py:14
  166.5 11.2 %all-to-all-done.5 = f32[16,1,4096]{2,1,0:T(1,128)S(1)} async-done(((f32[16,1,4096]{2,1,0:T(1,128)}), f32[16,1,4096]{2,1,0:T(1,128)S(1)}, u32[]{:S(2)}, u32[]{:S(2)}) %all-to-all-start.5) | async-done | bytes 262176 | tf_op jit(solution)/shard_map/all_to_all | solution.py:14
  178.9 5.6 %all-to-all-start.7 = ((f32[32,1,128]{2,1,0:T(1,128)}), f32[32,1,128]{2,1,0:T(1,128)S(1)}, u32[]{:S(2)}, u32[]{:S(2)}) async-start(f32[32,1,128]{2,1,0:T(1,128)} %broadcast_in_dim.44), calls=%async_computation.7 | async-start | bytes 32768 | tf_op jit(solution)/shard_map/all_to_all | solution.py:14
  184.4 8.1 %fusion.3 = f32[128,1024]{0,1:T(8,128)} fusion(bf16[4096,1024]{1,0:T(8,128)(2,1)} %param.5, f32[4096]{0:T(1024)S(1)} %get-tuple-element.19, s32[4096]{0:T(1024)S(1)} %bitcast.44), kind=kOutput, calls=%fused_computation.6 | convolution fusion | flops 1086849024 | bytes 8945664 | tf_op jit(solution)/shard_map/dot_general | solution.py:101
  192.9 9.4 %all-to-all-start.6 = ((f32[32,128,32]{1,2,0:T(8,128)}), f32[32,128,32]{1,2,0:T(8,128)S(1)}, u32[]{:S(2)}, u32[]{:S(2)}) async-start(f32[32,128,32]{1,2,0:T(8,128)} %bitcast.10), calls=%async_computation.6 | async-start | bytes 1048576 | tf_op jit(solution)/shard_map/all_to_all | solution.py:34
  202.5 16.8 %all-to-all-done.6 = f32[32,128,32]{1,2,0:T(8,128)S(1)} async-done(((f32[32,128,32]{1,2,0:T(8,128)}), f32[32,128,32]{1,2,0:T(8,128)S(1)}, u32[]{:S(2)}, u32[]{:S(2)}) %all-to-all-start.6) | async-done | bytes 524320 | tf_op jit(solution)/shard_map/all_to_all | solution.py:34
  219.8 11.4 %all_to_all.71 = f32[16,1,2112]{2,1,0:T(1,128)S(1)} all-to-all(f32[16,1,2112]{2,1,0:T(1,128)S(1)} %broadcast_in_dim.45), channel_id=1, replica_groups=mesh['pts'=32,'cen'=16] {'cen'}, dimensions={0} | all-to-all | bytes 270336 | tf_op jit(solution)/shard_map/all_to_all | solution.py:14
  232.6 5.6 %all-to-all-start.9 = ((f32[32,32,192]{2,1,0:T(8,128)}), f32[32,32,192]{2,1,0:T(8,128)S(1)}, u32[]{:S(2)}, u32[]{:S(2)}) async-start(f32[32,32,192]{2,1,0:T(8,128)} %stack.7), calls=%async_computation.9 | async-start | bytes 2097152 | tf_op jit(solution)/shard_map/all_to_all | solution.py:51
  238.8 28.2 %all-to-all-done.9 = f32[32,32,192]{2,1,0:T(8,128)S(1)} async-done(((f32[32,32,192]{2,1,0:T(8,128)}), f32[32,32,192]{2,1,0:T(8,128)S(1)}, u32[]{:S(2)}, u32[]{:S(2)}) %all-to-all-start.9) | async-done | bytes 786464 | tf_op jit(solution)/shard_map/all_to_all | solution.py:51
  (65 shorter events, 13.3 us)
Async XLA Ops:
  0.6 75.3 %copy-start = (f32[64,1024]{1,0:T(8,128)S(1)}, f32[64,1024]{1,0:T(8,128)}, u32[]{:S(2)}) copy-start(f32[64,1024]{1,0:T(8,128)} %param.8) | copy-start | bytes 786436
  31.7 14.9 %all-to-all-start = ((f32[16,1,4096]{2,1,0:T(1,128)}), f32[16,1,4096]{2,1,0:T(1,128)S(1)}, u32[]{:S(2)}, u32[]{:S(2)}) async-start(f32[16,1,4096]{2,1,0:T(1,128)} %broadcast_in_dim.38), calls=%async_computation | async-start | bytes 524288 | tf_op jit(solution)/shard_map/all_to_all | solution.py:14
  47.7 18.7 %all-to-all-start.2 = ((f32[32,1,128]{2,1,0:T(1,128)}), f32[32,1,128]{2,1,0:T(1,128)S(1)}, u32[]{:S(2)}, u32[]{:S(2)}) async-start(f32[32,1,128]{2,1,0:T(1,128)} %broadcast_in_dim.40), calls=%async_computation.2 | async-start | bytes 32768 | tf_op jit(solution)/shard_map/all_to_all | solution.py:14
  58.0 18.0 %copy-start.1 = (s32[128]{0:T(128)S(1)}, s32[128]{0:T(128)}, u32[]{:S(2)}) copy-start(s32[128]{0:T(128)} %param.9) | copy-start | bytes 1540
  66.5 26.4 %all-to-all-start.1 = ((f32[32,128,32]{1,2,0:T(8,128)}), f32[32,128,32]{1,2,0:T(8,128)S(1)}, u32[]{:S(2)}, u32[]{:S(2)}) async-start(f32[32,128,32]{1,2,0:T(8,128)} %bitcast.3), calls=%async_computation.1 | async-start | bytes 1048576 | tf_op jit(solution)/shard_map/all_to_all | solution.py:34
  94.1 12.3 %all-to-all-start.3 = ((f32[16,1,2112]{2,1,0:T(1,128)}), f32[16,1,2112]{2,1,0:T(1,128)S(1)}, u32[]{:S(2)}, u32[]{:S(2)}) async-start(f32[16,1,2112]{2,1,0:T(1,128)} %broadcast_in_dim.41), calls=%async_computation.3 | async-start | bytes 278528 | tf_op jit(solution)/shard_map/all_to_all | solution.py:14
  162.8 14.9 %all-to-all-start.5 = ((f32[16,1,4096]{2,1,0:T(1,128)}), f32[16,1,4096]{2,1,0:T(1,128)S(1)}, u32[]{:S(2)}, u32[]{:S(2)}) async-start(f32[16,1,4096]{2,1,0:T(1,128)} %broadcast_in_dim.42), calls=%async_computation.5 | async-start | bytes 524288 | tf_op jit(solution)/shard_map/all_to_all | solution.py:14
  178.9 14.1 %all-to-all-start.7 = ((f32[32,1,128]{2,1,0:T(1,128)}), f32[32,1,128]{2,1,0:T(1,128)S(1)}, u32[]{:S(2)}, u32[]{:S(2)}) async-start(f32[32,1,128]{2,1,0:T(1,128)} %broadcast_in_dim.44), calls=%async_computation.7 | async-start | bytes 32768 | tf_op jit(solution)/shard_map/all_to_all | solution.py:14
  192.9 26.4 %all-to-all-start.6 = ((f32[32,128,32]{1,2,0:T(8,128)}), f32[32,128,32]{1,2,0:T(8,128)S(1)}, u32[]{:S(2)}, u32[]{:S(2)}) async-start(f32[32,128,32]{1,2,0:T(8,128)} %bitcast.10), calls=%async_computation.6 | async-start | bytes 1048576 | tf_op jit(solution)/shard_map/all_to_all | solution.py:34
  232.6 34.4 %all-to-all-start.9 = ((f32[32,32,192]{2,1,0:T(8,128)}), f32[32,32,192]{2,1,0:T(8,128)S(1)}, u32[]{:S(2)}, u32[]{:S(2)}) async-start(f32[32,32,192]{2,1,0:T(8,128)} %stack.7), calls=%async_computation.9 | async-start | bytes 2097152 | tf_op jit(solution)/shard_map/all_to_all | solution.py:51
